TPU v7x, 32 devices: a whole 2x2x4 slice. The times are simulated.
32 devices in a mesh: dp: 8 (over z, y), head: 4 (over x, core).
Axes of the slice: x: 2, y: 2, z: 4, core: 2. Of those that a mesh axis runs over, the one named last changes fastest.
Arguments:
- tokens: bfloat16 [32768, 768], P(('dp', 'head')), may hold values from -6 to 6
- seq_lengths: int32 [64, 32], P('dp'), may hold values from 0 to 512, as said below
- qkv_weight: bfloat16 [2, 3, 768, 768], P(None, None, None, 'head'), may hold values from -0.21875 to 0.21875
- qv_bias: float32 [2, 2, 768], P(None, None, 'head'), may hold values from -3 to 3
- out_weight: bfloat16 [2, 768, 768], replicated, may hold values from -0.875 to 0.875
- out_bias: float32 [2, 768], replicated, may hold values from -3 to 3
- norm1_gain: float32 [2, 768], replicated, may hold values from 0.25 to 1.75
- norm1_shift: float32 [2, 768], replicated, may hold values from -3 to 3
- up_weight: bfloat16 [2, 768, 3072], replicated, may hold values from -0.21875 to 0.21875
- up_bias: float32 [2, 3072], replicated, may hold values from -3 to 3
- down_weight: bfloat16 [2, 3072, 768], replicated, may hold values from -0.109375 to 0.109375
- down_bias: float32 [2, 768], replicated, may hold values from -3 to 3
- norm2_gain: float32 [2, 768], replicated, may hold values from 0.25 to 1.75
- norm2_shift: float32 [2, 768], replicated, may hold values from -3 to 3
- out_grad: bfloat16 [32768, 768], P(('dp', 'head')), may hold values from -6 to 6
Outputs:
- out_state: bfloat16 [32768, 768], P(('dp', 'head'))
- input_grad: bfloat16 [32768, 768], P(('dp', 'head'))
- qkv_weight_grad: float32 [2, 3, 768, 768], P(None, None, 'dp', 'head')
- qv_bias_grad: float32 [2, 2, 768], replicated
- out_weight_grad: float32 [2, 768, 768], P(None, 'dp', 'head')
- out_bias_grad: float32 [2, 768], replicated
- norm1_gain_grad: float32 [2, 768], replicated
- norm1_shift_grad: float32 [2, 768], replicated
- up_weight_grad: float32 [2, 768, 3072], P(None, 'dp', 'head')
- up_bias_grad: float32 [2, 3072], replicated
- down_weight_grad: float32 [2, 3072, 768], P(None, 'head', 'dp')
- down_bias_grad: float32 [2, 768], replicated
- norm2_gain_grad: float32 [2, 768], replicated
- norm2_shift_grad: float32 [2, 768], replicated
Inputs may be any that keep to these rules, and one draw needn't show every extreme that they name: `seq_lengths`: each slot's row sums to 512; nonzero entries come first and zero entries mark no sequence; some slot holds a single sequence of 512 rows.
All inputs are finite; a program needn't handle non-finite values.
Results may differ from a plain program's by a relative error of at most 0.025.
Values may be sent and summed in bfloat16 or wider, within the bound.
No kernel may reach another device: no remote copies, remote signals or barrier semaphores. Data moves between devices by JAX's collectives and lax.ppermute only.
A program may use at most 256 MiB of HBM per device.

v0:
```python
import jax
import jax.numpy as jnp
from jax import lax
from jax.sharding import PartitionSpec as P

HD = 64
EPSILON = 1e-06


def norm_rows(values, gain, shift):
    centre = jnp.mean(values, axis=-1, keepdims=True)
    centred = values - centre
    spread = jnp.mean(centred * centred, axis=-1, keepdims=True)
    return centred * lax.rsqrt(spread + EPSILON) * gain + shift


def exact_gelu(values):
    return jax.nn.gelu(values, approximate=False)


def segment_ids(lengths, slot_rows):
    boundary = jnp.cumsum(lengths, axis=1)
    position = jnp.arange(slot_rows, dtype=jnp.int32)
    return jnp.sum((position[None, :, None] >= boundary[:, None, :]).astype(jnp.int32), axis=2)


def slot_scores(queries, keys_in, segments):
    scaling = queries.shape[-1] ** (-0.5)
    scores = (
        jnp.einsum("qhd,khd->hqk", queries, keys_in, preferred_element_type=jnp.float32) * scaling
    )
    inside = (segments[:, None] == segments[None, :])[None]
    return (scores, inside)


def slot_forward(packed):
    queries, keys_in, values_in, segments = packed
    scores, inside = slot_scores(queries, keys_in, segments)
    scores = jnp.where(inside, scores, -1e30)
    peak_score = jnp.max(scores, axis=-1, keepdims=True)
    weights = jnp.exp(scores - peak_score)
    denominator = jnp.sum(weights, axis=-1, keepdims=True)
    probability = (weights / denominator).astype(jnp.bfloat16)
    context = jnp.einsum("hqk,khd->qhd", probability, values_in, preferred_element_type=jnp.float32)
    return (context.astype(jnp.bfloat16), (peak_score + jnp.log(denominator))[..., 0])


def slot_backward(packed):
    queries, keys_in, values_in, grad_context, log_total, segments = packed
    scaling = queries.shape[-1] ** (-0.5)
    scores, inside = slot_scores(queries, keys_in, segments)
    probability = jnp.where(inside, jnp.exp(scores - log_total[..., None]), 0.0)
    grad_prob = jnp.einsum(
        "qhd,khd->hqk", grad_context, values_in, preferred_element_type=jnp.float32
    )
    shares = jnp.sum(probability * grad_prob, axis=-1, keepdims=True)
    grad_score = (probability * (grad_prob - shares)).astype(jnp.bfloat16)
    grad_query = (
        jnp.einsum("hqk,khd->qhd", grad_score, keys_in, preferred_element_type=jnp.float32)
        * scaling
    )
    grad_key = (
        jnp.einsum("hqk,qhd->khd", grad_score, queries, preferred_element_type=jnp.float32)
        * scaling
    )
    grad_value = jnp.einsum(
        "hqk,qhd->khd",
        probability.astype(jnp.bfloat16),
        grad_context,
        preferred_element_type=jnp.float32,
    )
    return (
        grad_query.astype(jnp.bfloat16),
        grad_key.astype(jnp.bfloat16),
        grad_value.astype(jnp.bfloat16),
    )


def on_device(
    tokens,
    seq_lengths,
    qkv_weight,
    qv_bias,
    out_weight,
    out_bias,
    norm1_gain,
    norm1_shift,
    up_weight,
    up_bias,
    down_weight,
    down_bias,
    norm2_gain,
    norm2_shift,
    out_grad,
):
    heads_count = lax.axis_size("head")
    head_index = lax.axis_index("head")
    local_rows, model_width = tokens.shape
    group_rows = local_rows * heads_count
    slots_here = seq_lengths.shape[0]
    slot_rows = group_rows // slots_here
    segments = segment_ids(seq_lengths, slot_rows)
    head_width = qkv_weight.shape[-1]
    local_heads = head_width // HD
    layers = qkv_weight.shape[0]
    qkv_shape = (slots_here, slot_rows, 3, local_heads, HD)
    hidden_state = tokens.astype(jnp.float32)
    kept_values = []
    for layer_index in range(layers):
        gathered = lax.all_gather(hidden_state.astype(jnp.bfloat16), "head", axis=0, tiled=True)
        projected = jnp.einsum(
            "rd,cde->rce", gathered, qkv_weight[layer_index], preferred_element_type=jnp.float32
        )
        bias_rows = jnp.stack(
            [
                qv_bias[layer_index, 0],
                jnp.zeros_like(qv_bias[layer_index, 0]),
                qv_bias[layer_index, 1],
            ]
        )
        projected = (projected + bias_rows[None]).astype(jnp.bfloat16)
        shaped = projected.reshape(qkv_shape)
        context, log_total = lax.map(
            slot_forward, (shaped[:, :, 0], shaped[:, :, 1], shaped[:, :, 2], segments)
        )
        context = context.reshape(group_rows, head_width)
        token_context = lax.all_to_all(context, "head", split_axis=0, concat_axis=1, tiled=True)
        attended = (
            jnp.dot(token_context, out_weight[layer_index], preferred_element_type=jnp.float32)
            + out_bias[layer_index]
        )
        first_sum = hidden_state + attended
        normed = norm_rows(first_sum, norm1_gain[layer_index], norm1_shift[layer_index])
        normed_low = normed.astype(jnp.bfloat16)
        ffn_rows = normed_low
        up_part = up_weight[layer_index]
        up_shift = up_bias[layer_index]
        down_part = down_weight[layer_index]
        before_gelu = jnp.dot(ffn_rows, up_part, preferred_element_type=jnp.float32) + up_shift
        activated = exact_gelu(before_gelu).astype(jnp.bfloat16)
        branch = jnp.dot(activated, down_part, preferred_element_type=jnp.float32)
        second_sum = normed + branch + down_bias[layer_index]
        hidden_state = norm_rows(second_sum, norm2_gain[layer_index], norm2_shift[layer_index])
        kept_values.append(
            (
                gathered,
                projected,
                log_total,
                token_context,
                first_sum,
                ffn_rows,
                up_part,
                down_part,
                before_gelu,
                activated,
                second_sum,
            )
        )
    out_state = hidden_state.astype(jnp.bfloat16)
    grad_state = out_grad.astype(jnp.float32)
    ffn_list, proj_list, attn_list, small_list, shift_list = ([], [], [], [], [])
    for layer_index in reversed(range(layers)):
        (
            gathered,
            projected,
            log_total,
            token_context,
            first_sum,
            ffn_rows,
            up_part,
            down_part,
            before_gelu,
            activated,
            second_sum,
        ) = kept_values[layer_index]
        pull_second = jax.vjp(
            norm_rows, second_sum, norm2_gain[layer_index], norm2_shift[layer_index]
        )[1]
        grad_second, grad_gain2, grad_shift2 = pull_second(grad_state)
        grad_branch = grad_second.astype(jnp.bfloat16)
        grad_down_shift = jnp.sum(grad_branch.astype(jnp.float32), axis=0)
        grad_down = jnp.einsum(
            "rd,rf->df", grad_branch, activated, preferred_element_type=jnp.float32
        )
        grad_act = jnp.einsum(
            "rd,fd->rf", grad_branch, down_part, preferred_element_type=jnp.float32
        )
        pull_gelu = jax.vjp(exact_gelu, before_gelu)[1]
        grad_pre = pull_gelu(grad_act)[0].astype(jnp.bfloat16)
        grad_up_shift = jnp.sum(grad_pre.astype(jnp.float32), axis=0)
        grad_up = jnp.einsum("rd,rf->df", ffn_rows, grad_pre, preferred_element_type=jnp.float32)
        grad_normed_low = jnp.einsum(
            "rf,df->rd", grad_pre, up_part, preferred_element_type=jnp.float32
        )
        grad_normed = grad_second + grad_normed_low
        pull_first = jax.vjp(
            norm_rows, first_sum, norm1_gain[layer_index], norm1_shift[layer_index]
        )[1]
        grad_first, grad_gain1, grad_shift1 = pull_first(grad_normed)
        grad_attended = grad_first.astype(jnp.bfloat16)
        grad_out_shift = jnp.sum(grad_attended.astype(jnp.float32), axis=0)
        grad_out = jnp.einsum(
            "rd,re->de", token_context, grad_attended, preferred_element_type=jnp.float32
        )
        grad_mixed = jnp.einsum(
            "re,de->rd", grad_attended, out_weight[layer_index], preferred_element_type=jnp.float32
        ).astype(jnp.bfloat16)
        grad_context = lax.all_to_all(grad_mixed, "head", split_axis=1, concat_axis=0, tiled=True)
        shaped = projected.reshape(qkv_shape)
        grad_query, grad_key, grad_value = lax.map(
            slot_backward,
            (
                shaped[:, :, 0],
                shaped[:, :, 1],
                shaped[:, :, 2],
                grad_context.reshape(slots_here, slot_rows, local_heads, HD),
                log_total,
                segments,
            ),
        )
        grad_proj = jnp.stack([grad_query, grad_key, grad_value], axis=2).reshape(
            group_rows, 3, head_width
        )
        grad_qkv = jnp.einsum(
            "rd,rce->cde", gathered, grad_proj, preferred_element_type=jnp.float32
        )
        bias_local = jnp.sum(grad_proj.astype(jnp.float32), axis=0)
        qv_local = jnp.stack([bias_local[0], bias_local[2]])
        qv_full = lax.dynamic_update_slice_in_dim(
            jnp.zeros((2, model_width), jnp.float32), qv_local, head_index * head_width, 1
        )
        layer_weights = qkv_weight[layer_index]
        grad_state = grad_first + lax.psum_scatter(
            jnp.einsum(
                "rce,cde->rd", grad_proj, layer_weights, preferred_element_type=jnp.float32
            ).astype(jnp.bfloat16),
            "head",
            scatter_dimension=0,
            tiled=True,
        ).astype(jnp.float32)
        ffn_list.append(jnp.stack([grad_up, grad_down]))
        proj_list.append(grad_out)
        attn_list.append(grad_qkv)
        small_list.append(
            jnp.concatenate(
                [
                    qv_full,
                    jnp.stack(
                        [
                            grad_out_shift,
                            grad_gain1,
                            grad_shift1,
                            grad_down_shift,
                            grad_gain2,
                            grad_shift2,
                        ]
                    ),
                ],
                axis=0,
            )
        )
        shift_list.append(grad_up_shift)
    input_grad = grad_state.astype(jnp.bfloat16)
    ffn_stack = jnp.stack(ffn_list[::-1])
    proj_stack = jnp.stack(proj_list[::-1])
    attn_stack = jnp.stack(attn_list[::-1])
    small_stack = jnp.stack(small_list[::-1])
    shift_stack = jnp.stack(shift_list[::-1])
    ffn_data, proj_data, attn_data = (
        lax.psum_scatter(
            ffn_stack.astype(jnp.bfloat16), "dp", scatter_dimension=2, tiled=True
        ).astype(jnp.float32),
        lax.psum_scatter(
            proj_stack.astype(jnp.bfloat16), "dp", scatter_dimension=1, tiled=True
        ).astype(jnp.float32),
        lax.psum_scatter(
            attn_stack.astype(jnp.bfloat16), "dp", scatter_dimension=2, tiled=True
        ).astype(jnp.float32),
    )
    ffn_head, proj_head = (
        lax.psum_scatter(
            ffn_data.astype(jnp.bfloat16), "head", scatter_dimension=3, tiled=True
        ).astype(jnp.float32),
        lax.psum_scatter(
            proj_data.astype(jnp.bfloat16), "head", scatter_dimension=2, tiled=True
        ).astype(jnp.float32),
    )
    small_sum, shift_sum = lax.psum((small_stack, shift_stack), ("dp", "head"))
    down_weight_grad = jnp.transpose(ffn_head[:, 1], (0, 2, 1))
    return (
        out_state,
        input_grad,
        attn_data,
        small_sum[:, 0:2],
        proj_head,
        small_sum[:, 2],
        small_sum[:, 3],
        small_sum[:, 4],
        ffn_head[:, 0],
        shift_sum,
        down_weight_grad,
        small_sum[:, 5],
        small_sum[:, 6],
        small_sum[:, 7],
    )


def solution(mesh):
    in_specs = (
        P(("dp", "head"), None),
        P("dp", None),
        P(None, None, None, "head"),
        P(None, None, "head"),
        P(),
        P(),
        P(),
        P(),
        P(),
        P(),
        P(),
        P(),
        P(),
        P(),
        P(("dp", "head"), None),
    )
    out_specs = (
        P(("dp", "head"), None),
        P(("dp", "head"), None),
        P(None, None, "dp", "head"),
        P(),
        P(None, "dp", "head"),
        P(),
        P(),
        P(),
        P(None, "dp", "head"),
        P(),
        P(None, "head", "dp"),
        P(),
        P(),
        P(),
    )
    return jax.shard_map(
        on_device, mesh=mesh, in_specs=in_specs, out_specs=out_specs, check_vma=False
    )
```

profile of v0, /device:TPU:0, one launch (start us, length us, event | category | flops | bytes accessed | tf_op | source)
XLA Modules:
  0.0 1406.1 jit_solution(3311266776964060774)
XLA Ops:
  12.9 45.8 %all-gather.3.cloned.1.call-done = bf16[4096,768]{1,0:T(8,128)(2,1)} async-done(((bf16[1024,768]{1,0:T(8,128)(2,1)}), bf16[4096,768]{1,0:T(8,128)(2,1)}) %all-gather.3.cloned.1.call-update) | async-done | bytes 6291472 | tf_op jit(solution)/shard_map/all_gather | solution.py:110
  58.7 6.0 fusion.216
  73.9 35.4 %while.52 = (s32[]{:T(128)}, bf16[8,512,3,64]{1,3,2,0:T(8,128)(2,1)}, f32[8,3,512]{2,1,0:T(4,128)S(1)}, bf16[8,512,3,64]{1,3,2,0:T(8,128)(2,1)}, s32[8,512]{1,0:...) while((s32[]{:T(128)}, ...), condition=%wide.region_5.6_spmd, body=%wide.region_2.5_spmd.sunk | while | flops 211122688 | bytes 11335773 | solution.py:123
  109.2 4.6 copy.159
  113.8 13.7 all_to_all.52
  130.6 3.7 all-to-all-start
  139.1 15.2 %all-to-all-done = bf16[4,1024,192]{1,2,0:T(8,128)(2,1)S(1)} async-done(((bf16[4,1024,192]{1,2,0:T(8,128)(2,1)}), bf16[4,1024,192]{1,2,0:T(8,128)(2,1)S(1)}, u32[]{:S(2)}, u32[]{:S(2)}) %all-to-all-start) | async-done | bytes 1572896 | tf_op jit(solution)/shard_map/all_to_all | solution.py:127
  154.4 4.0 fusion.212
  158.9 38.8 %multiply_convert_fusion.3 = (bf16[1024,3072]{1,0:T(8,128)(2,1)}, f32[1024,3072]{1,0:T(8,128)}, f32[1024,3072]{1,0:T(8,128)}) fusion(f32[3072]{0:T(1024)S(1)} %bitcast.494, bf16[2,768,3072]{2,1,0:T(8,128)(2,1)} %param.31, f32[1024,768]{0,1:T(8,128)S(1)} %get-tuple-element.478, f32[768]{0:T(1024)S(1)} %get-tuple-element.347, ...), kind=kOutput, calls=%fused_computation.148 | convolution fusion | flops 5043388416 | bytes 39348224 | tf_op jit(solution)/shard_map/dot_general | solution.py:139
  197.8 8.6 fusion.213
  208.6 46.5 %all-gather.5.cloned.1.call-done = bf16[4096,768]{0,1:T(8,128)(2,1)} async-done(((bf16[1024,768]{0,1:T(8,128)(2,1)}), bf16[4096,768]{0,1:T(8,128)(2,1)}) %all-gather.5.cloned.1.call-update) | async-done | bytes 6291472 | tf_op jit(solution)/shard_map/all_gather | solution.py:110
  255.2 6.6 fusion.217
  273.1 43.5 %while.53 = (s32[]{:T(128)}, bf16[8,512,3,64]{1,3,2,0:T(8,128)(2,1)}, f32[8,3,512]{2,1,0:T(4,128)S(1)}, bf16[8,512,3,64]{1,3,2,0:T(8,128)(2,1)}, s32[8,512]{1,0:...) while((s32[]{:T(128)}, ...), condition=%wide.region_13.14_spmd, body=%wide.region_10.13_spmd.sunk | while | flops 211122688 | bytes 11335773 | solution.py:123
  316.7 3.5 copy.165
  320.1 3.7 all_to_all.56
  323.9 3.2 copy.166
  327.0 4.6 all-to-all-start.1
  334.3 17.5 %all-to-all-done.1 = bf16[4,1024,192]{1,2,0:T(8,128)(2,1)} async-done(((bf16[4,1024,192]{1,2,0:T(8,128)(2,1)}), bf16[4,1024,192]{1,2,0:T(8,128)(2,1)}, u32[]{:S(2)}, u32[]{:S(2)}) %all-to-all-start.1) | async-done | bytes 1572896 | tf_op jit(solution)/shard_map/all_to_all | solution.py:127
  351.9 3.8 fusion.214
  356.5 38.4 %multiply_convert_fusion.2 = (bf16[1024,3072]{1,0:T(8,128)(2,1)}, f32[1024,3072]{1,0:T(8,128)}, f32[1024,3072]{1,0:T(8,128)}) fusion(f32[3072]{0:T(1024)S(1)} %bitcast.497, bf16[2,768,3072]{2,1,0:T(8,128)(2,1)} %param.31, f32[1024,768]{0,1:T(8,128)S(1)} %get-tuple-element.483, f32[768]{0:T(1024)S(1)} %copy-done.73, f32[768]{0:T(1024)S(1)} %copy-done.52, ...), kind=kOutput, calls=%fused_computation.135 | convolution fusion | flops 5043388416 | bytes 39348224 | tf_op jit(solution)/shard_map/dot_general | solution.py:139
  395.0 8.9 fusion.215
  407.8 3.3 convert_reduce_fusion.5
  411.1 18.2 %convert_reduce_fusion = (f32[3072]{0:T(1024)}, bf16[1024,3072]{1,0:T(8,128)(2,1)}) fusion(f32[1024,3072]{1,0:T(8,128)} %get-tuple-element.435, bf16[1024,768]{0,1:T(8,128)(2,1)S(1)} %get-tuple-element.425, bf16[2,3072,768]{2,1,0:T(8,128)(2,1)} %param.33, f32[1024,3072]{1,0:T(8,128)} %get-tuple-element.484, f32[3072]{0:T(1024)S(1)} %bitcast.498), kind=kOutput, calls=%fused_computation.131 | convolution fusion | flops 4885312512 | bytes 37773312 | tf_op jit(solution)/shard_map/rd,fd->rf/dot_general | solution.py:185
  429.4 11.7 multiply_reduce_fusion.2
  447.9 3.6 all-to-all-start.2
  451.5 20.0 %all-to-all-done.2 = bf16[1024,4,192]{0,2,1:T(8,128)(2,1)S(1)} async-done(((bf16[1024,4,192]{0,2,1:T(8,128)(2,1)}), bf16[1024,4,192]{0,2,1:T(8,128)(2,1)S(1)}, u32[]{:S(2)}, u32[]{:S(2)}) %all-to-all-start.2) | async-done | bytes 1572896 | tf_op jit(solution)/shard_map/all_to_all | solution.py:208
  479.6 88.1 %while.54 = (s32[]{:T(128)}, bf16[8,512,3,64]{1,3,2,0:T(8,128)(2,1)S(1)}, bf16[8,512,3,64]{1,3,2,0:T(8,128)(2,1)}, bf16[8,512,3,64]{1,3,2,0:T(8,128)(2,1)}, bf16...) while((s32[]{:T(128)}, ...), condition=%wide.region_24.25_spmd, body=%wide.region_22.24_spmd.sunk | while | flops 511146496 | bytes 26125428 | solution.py:210
  575.4 3.4 copy.174
  583.9 9.5 bitcast_convert_fusion.1
  594.8 4.0 fusion.172
  598.8 11.7 fusion.140
  610.5 41.4 %reduce-scatter.12.cloned.1.call-done = bf16[1024,768]{0,1:T(8,128)(2,1)} async-done(((bf16[4096,768]{0,1:T(8,128)(2,1)}), bf16[1024,768]{0,1:T(8,128)(2,1)}) %reduce-scatter.12.cloned.1.call-update) | async-done | bytes 1572880 | tf_op jit(solution)/shard_map/reduce_scatter | solution.py:233
  651.9 3.9 multiply_reduce_fusion.3
  659.1 18.5 %convert_reduce_fusion.1 = (f32[3072]{0:T(1024)S(1)}, bf16[1024,3072]{1,0:T(8,128)(2,1)}) fusion(f32[1024,3072]{1,0:T(8,128)} %get-tuple-element.437, bf16[1024,768]{0,1:T(8,128)(2,1)} %get-tuple-element.421, bf16[2,3072,768]{2,1,0:T(8,128)(2,1)} %param.33, f32[1024,3072]{1,0:T(8,128)} %get-tuple-element.479, f32[3072]{0:T(1024)S(1)} %bitcast.495), kind=kOutput, calls=%fused_computation.132 | convolution fusion | flops 4885312512 | bytes 37773312 | tf_op jit(solution)/shard_map/rd,fd->rf/dot_general | solution.py:185
  677.7 9.9 multiply_reduce_fusion.4
  693.2 9.0 fusion.141
  702.3 8.4 maximum_bitcast_fusion.1
  710.6 9.3 fusion.139
  719.9 9.8 fusion.138
  729.7 8.3 maximum_bitcast_fusion
  738.1 16.7 %pad_maximum_fusion = bf16[2,2,768,3072]{3,2,1,0:T(8,128)(2,1)} fusion(bf16[1,2,768,3072]{3,2,1,0:T(8,128)(2,1)} %maximum_bitcast_fusion.1, bf16[1,2,768,3072]{3,2,1,0:T(8,128)(2,1)} %maximum_bitcast_fusion), kind=kLoop, calls=%fused_computation.126 | loop fusion | flops 9437184 | bytes 37748736 | tf_op jit(solution)/shard_map/stack | solution.py:264
  758.9 4.3 convolution_convert_fusion.4
  763.2 4.3 all-to-all-start.3
  768.0 9.0 fusion.173
  777.7 10.0 all-to-all-done.3
  787.7 3.8 copy.177
  791.5 3.6 reshape.394
  802.2 101.9 %while.55 = (s32[]{:T(128)}, bf16[8,512,3,64]{1,3,2,0:T(8,128)(2,1)}, bf16[8,512,3,64]{1,3,2,0:T(8,128)(2,1)}, bf16[8,512,3,64]{1,3,2,0:T(8,128)(2,1)}, bf16[8,5...) while((s32[]{:T(128)}, ...), condition=%wide.region_32.33_spmd, body=%wide.region_30.32_spmd.sunk | while | flops 511146496 | bytes 26125428 | solution.py:210
  904.1 3.4 copy.179
  907.5 3.7 stack.140
  911.2 3.5 copy.180
  914.7 3.8 stack.141
  918.5 3.4 copy.181
  921.9 3.8 stack.142
  932.2 8.1 fusion.176
  941.8 5.9 copy.207
  947.7 6.9 reshape.411
  957.0 9.7 bitcast_convert_fusion
  966.8 112.1 %reduce-scatter.18.cloned.1.call-done = bf16[2,2,96,3072]{3,2,1,0:T(8,128)(2,1)} async-done(((bf16[2,2,768,3072]{3,2,1,0:T(8,128)(2,1)}), bf16[2,2,96,3072]{3,2,1,0:T(8,128)(2,1)}) %reduce-scatter.18.cloned.1.call-update) | async-done | bytes 2359312 | tf_op jit(solution)/shard_map/reduce_scatter | solution.py:270
  1081.6 122.8 %all-reduce.3.cloned.1.call-done = (f32[2,8,768]{2,0,1:T(2,128)}, f32[2,3072]{1,0:T(2,128)}) async-done(((f32[2,8,768]{2,0,1:T(2,128)}, f32[2,3072]{1,0:T(2,128)}), (f32[2,8,768]{2,0,1:T(2,128)}, f32[2,3072]{1,0:T(2,128)})) %all-reduce.3.cloned.1.call-update) | async-done | bytes 73744 | tf_op jit(solution)/shard_map/psum | solution.py:288
  1207.1 69.8 %reduce-scatter.22.cloned.1.call-done = bf16[96,1152]{1,0:T(8,128)(2,1)} async-done(((bf16[768,1152]{1,0:T(8,128)(2,1)}), bf16[96,1152]{1,0:T(8,128)(2,1)}) %reduce-scatter.22.cloned.1.call-update) | async-done | bytes 221200
  1281.1 18.6 %reduce-scatter.24.cloned.1.call-done = bf16[192,192]{1,0:T(8,128)(2,1)} async-done(((bf16[768,192]{1,0:T(8,128)(2,1)}), bf16[192,192]{1,0:T(8,128)(2,1)}) %reduce-scatter.24.cloned.1.call-update) | async-done | bytes 73744
  1301.4 59.1 %reduce-scatter.14.cloned.1.call-done = bf16[1024,768]{0,1:T(8,128)(2,1)} async-done(((bf16[4096,768]{0,1:T(8,128)(2,1)}), bf16[1024,768]{0,1:T(8,128)(2,1)}) %reduce-scatter.14.cloned.1.call-update) | async-done | bytes 1572880 | tf_op jit(solution)/shard_map/reduce_scatter | solution.py:233
  1366.3 29.9 %reduce-scatter.20.cloned.1.call-done = bf16[2,2,96,768]{3,2,1,0:T(8,128)(2,1)} async-done(((bf16[2,2,96,3072]{3,2,1,0:T(8,128)(2,1)}), bf16[2,2,96,768]{3,2,1,0:T(8,128)(2,1)}) %reduce-scatter.20.cloned.1.call-update) | async-done | bytes 589840 | tf_op jit(solution)/shard_map/reduce_scatter | solution.py:281
  (559 shorter events, 392.3 us)
Async XLA Ops:
  7.2 51.5 %all-gather.3.cloned.1.call-start = ((), (), s32[]{:S(2)}) async-start(), calls=%async_computation.11 | async-start | bytes 7864320 | tf_op jit(solution)/shard_map/all_gather | solution.py:110
  109.2 18.3 %copy-start.5 = (bf16[8,512,3,64]{1,3,2,0:T(8,128)(2,1)}, bf16[8,512,3,64]{1,3,2,0:T(8,128)(2,1)S(1)}, u32[]{:S(2)}) copy-start(bf16[8,512,3,64]{1,3,2,0:T(8,128)(2,1)S(1)} %get-tuple-element.866) | copy-start | bytes 4718596
  109.2 18.3 %copy-start.6 = (bf16[8,512,3,64]{1,3,2,0:T(8,128)(2,1)}, bf16[8,512,3,64]{1,3,2,0:T(8,128)(2,1)S(1)}, u32[]{:S(2)}) copy-start(bf16[8,512,3,64]{1,3,2,0:T(8,128)(2,1)S(1)} %get-tuple-element.867) | copy-start | bytes 4718596
  109.2 18.3 %copy-start.31 = (f32[8,3,512]{2,1,0:T(4,128)}, f32[8,3,512]{2,1,0:T(4,128)S(1)}, u32[]{:S(2)}) copy-start(f32[8,3,512]{2,1,0:T(4,128)S(1)} %get-tuple-element.811) | copy-start | bytes 147460
  130.6 7.3 copy-start.69
  130.6 7.3 copy-start.70
  130.6 7.9 copy-start.48
  130.6 23.8 %all-to-all-start = ((bf16[4,1024,192]{1,2,0:T(8,128)(2,1)}), bf16[4,1024,192]{1,2,0:T(8,128)(2,1)S(1)}, u32[]{:S(2)}, u32[]{:S(2)}) async-start(bf16[4,1024,192]{1,2,0:T(8,128)(2,1)} %copy.160), calls=%async_computation | async-start | bytes 3145728 | tf_op jit(solution)/shard_map/all_to_all | solution.py:127
  134.3 120.8 %all-gather.5.cloned.1.call-start = ((), (), s32[]{:S(2)}) async-start(), calls=%async_computation.12 | async-start | bytes 7864320 | tf_op jit(solution)/shard_map/all_gather | solution.py:110
  137.9 59.8 %copy-start.50 = (f32[768]{0:T(1024)}, f32[768]{0:T(1024)S(1)}, u32[]{:S(2)}) copy-start(f32[768]{0:T(1024)S(1)} %get-tuple-element.495) | copy-start | bytes 9220
  137.9 59.8 %copy-start.71 = (f32[768]{0:T(1024)}, f32[768]{0:T(1024)S(1)}, u32[]{:S(2)}) copy-start(f32[768]{0:T(1024)S(1)} %get-tuple-element.347) | copy-start | bytes 9220
  138.5 213.3 %copy-start.35 = (f32[768]{0:T(1024)}, f32[768]{0:T(1024)S(1)}, u32[]{:S(2)}) copy-start(f32[768]{0:T(1024)S(1)} %get-tuple-element.497) | copy-start | bytes 9220
  139.1 19.7 %copy-start.61 = (f32[1,3072]{1,0:T(1,128)}, f32[1,3072]{1,0:T(1,128)S(1)}, u32[]{:S(2)}) copy-start(f32[1,3072]{1,0:T(1,128)S(1)} %get-tuple-element.464) | copy-start | bytes 36868
  154.4 43.4 %slice-start = ((s8[9437184]{0:T(1024)(128)(4,1)}), s8[4194304]{0:T(1024)(128)(4,1)S(1)}, s32[]{:S(2)}) async-start(s8[9437184]{0:T(1024)(128)(4,1)} %bitcast.500), calls=%async_computation.21 | async-start | bytes 8388608
  158.4 39.3 %copy-start.7 = (f32[1024,768]{0,1:T(8,128)}, f32[1024,768]{0,1:T(8,128)S(1)}, u32[]{:S(2)}) copy-start(f32[1024,768]{0,1:T(8,128)S(1)} %get-tuple-element.478) | copy-start | bytes 9437188
  158.4 39.3 %copy-start.40 = (f32[1024]{0:T(1024)}, f32[1024]{0:T(1024)S(1)}, u32[]{:S(2)}) copy-start(f32[1024]{0:T(1024)S(1)} %broadcast_multiply_fusion.3) | copy-start | bytes 12292
  158.8 38.8 %copy-start.42 = (f32[1024]{0:T(1024)}, f32[1024]{0:T(1024)S(1)}, u32[]{:S(2)}) copy-start(f32[1024]{0:T(1024)S(1)} %multiply_reduce_fusion.11) | copy-start | bytes 12292
  158.9 38.9 %copy-start.57 = (f32[1024]{0:T(1024)}, f32[1024]{0:T(1024)S(1)}, u32[]{:S(2)}) copy-start(f32[1024]{0:T(1024)S(1)} %fusion.189) | copy-start | bytes 12292
  158.9 38.9 %slice-start.1 = ((s8[9437184]{0:T(1024)(128)(4,1)}), s8[4194304]{0:T(1024)(128)(4,1)S(1)}, s32[]{:S(2)}) async-start(s8[9437184]{0:T(1024)(128)(4,1)} %bitcast.500), calls=%async_computation.22 | async-start | bytes 8388608
  158.9 38.9 %slice-start.2 = ((s8[9437184]{0:T(1024)(128)(4,1)}), s8[1048576]{0:T(1024)(128)(4,1)S(1)}, s32[]{:S(2)}) async-start(s8[9437184]{0:T(1024)(128)(4,1)} %bitcast.500), calls=%async_computation.23 | async-start | bytes 2097152
  206.4 145.4 %copy-start = (f32[1024,768]{0,1:T(8,128)}, f32[1024,768]{0,1:T(8,128)S(1)}, u32[]{:S(2)}) copy-start(f32[1024,768]{0,1:T(8,128)S(1)} %get-tuple-element.481) | copy-start | bytes 9437188
  206.4 145.4 %copy-start.33 = (f32[1024]{0:T(1024)}, f32[1024]{0:T(1024)S(1)}, u32[]{:S(2)}) copy-start(f32[1024]{0:T(1024)S(1)} %broadcast_multiply_fusion.2) | copy-start | bytes 12292
  206.8 145.0 %copy-start.37 = (f32[1024]{0:T(1024)}, f32[1024]{0:T(1024)S(1)}, u32[]{:S(2)}) copy-start(f32[1024]{0:T(1024)S(1)} %fusion.190) | copy-start | bytes 12292
  316.7 7.2 copy-start.30
  316.7 7.2 copy-start.32
  327.0 24.8 %copy-start.75 = (f32[768]{0:T(1024)S(1)}, f32[768]{0:T(1024)}, u32[]{:S(2)}) copy-start(f32[768]{0:T(1024)} %get-tuple-element.348) | copy-start | bytes 9220
  327.0 24.8 %all-to-all-start.1 = ((bf16[4,1024,192]{1,2,0:T(8,128)(2,1)}), bf16[4,1024,192]{1,2,0:T(8,128)(2,1)}, u32[]{:S(2)}, u32[]{:S(2)}) async-start(bf16[4,1024,192]{1,2,0:T(8,128)(2,1)} %copy.166), calls=%async_computation.1 | async-start | bytes 3145728 | tf_op jit(solution)/shard_map/all_to_all | solution.py:127
  351.8 43.1 %slice-start.3 = ((s8[9437184]{0:T(1024)(128)(4,1)}), s8[4194304]{0:T(1024)(128)(4,1)S(1)}, s32[]{:S(2)}) async-start(s8[9437184]{0:T(1024)(128)(4,1)} %bitcast.502), calls=%async_computation.24 | async-start | bytes 8388608
  355.7 39.3 %copy-start.10 = (f32[1024,768]{0,1:T(8,128)}, f32[1024,768]{0,1:T(8,128)S(1)}, u32[]{:S(2)}) copy-start(f32[1024,768]{0,1:T(8,128)S(1)} %get-tuple-element.483) | copy-start | bytes 9437188
  356.1 38.8 %copy-start.46 = (f32[1024]{0:T(1024)}, f32[1024]{0:T(1024)S(1)}, u32[]{:S(2)}) copy-start(f32[1024]{0:T(1024)S(1)} %multiply_reduce_fusion.9) | copy-start | bytes 12292
  356.5 38.5 %copy-start.74 = (f32[768]{0:T(1024)S(1)}, f32[768]{0:T(1024)}, u32[]{:S(2)}) copy-start(f32[768]{0:T(1024)} %get-tuple-element.342) | copy-start | bytes 9220
  356.5 38.5 %slice-start.4 = ((s8[9437184]{0:T(1024)(128)(4,1)}), s8[4194304]{0:T(1024)(128)(4,1)S(1)}, s32[]{:S(2)}) async-start(s8[9437184]{0:T(1024)(128)(4,1)} %bitcast.502), calls=%async_computation.25 | async-start | bytes 8388608
  356.5 38.5 %slice-start.5 = ((s8[9437184]{0:T(1024)(128)(4,1)}), s8[1048576]{0:T(1024)(128)(4,1)S(1)}, s32[]{:S(2)}) async-start(s8[9437184]{0:T(1024)(128)(4,1)} %bitcast.502), calls=%async_computation.26 | async-start | bytes 2097152
  395.0 8.9 copy-start.4
  395.0 8.9 copy-start.39
  411.1 18.2 %copy-start.24 = (bf16[1024,768]{0,1:T(8,128)(2,1)}, bf16[1024,768]{0,1:T(8,128)(2,1)S(1)}, u32[]{:S(2)}) copy-start(bf16[1024,768]{0,1:T(8,128)(2,1)S(1)} %get-tuple-element.425) | copy-start | bytes 4718596
  429.4 11.8 copy-start.47
  429.4 11.8 copy-start.11
  447.9 23.6 %all-to-all-start.2 = ((bf16[1024,4,192]{0,2,1:T(8,128)(2,1)}), bf16[1024,4,192]{0,2,1:T(8,128)(2,1)S(1)}, u32[]{:S(2)}, u32[]{:S(2)}) async-start(bf16[1024,4,192]{0,2,1:T(8,128)(2,1)} %bitcast.68), calls=%async_computation.2 | async-start | bytes 3145728 | tf_op jit(solution)/shard_map/all_to_all | solution.py:208
  451.4 200.5 %reduce-scatter.12.cloned.1.call-start = ((), (), s32[]{:S(2)}) async-start(), calls=%async_computation.13 | async-start | bytes 7864320 | tf_op jit(solution)/shard_map/reduce_scatter | solution.py:233
  593.4 361.3 %reduce-scatter.16.cloned.1.call-start = ((), (), s32[]{:S(2)}) async-start(), calls=%async_computation.15 | async-start | bytes 2654208 | tf_op jit(solution)/shard_map/reduce_scatter | solution.py:273
  598.8 53.1 %copy-start.1 = (f32[1024,768]{0,1:T(8,128)S(1)}, f32[1024,768]{0,1:T(8,128)}, u32[]{:S(2)}) copy-start(f32[1024,768]{0,1:T(8,128)} %copy-done) | copy-start | bytes 9437188
  598.8 53.1 %copy-start.34 = (f32[1024]{0:T(1024)S(1)}, f32[1024]{0:T(1024)}, u32[]{:S(2)}) copy-start(f32[1024]{0:T(1024)} %copy-done.33) | copy-start | bytes 12292
  598.8 53.1 %copy-start.36 = (f32[768]{0:T(1024)S(1)}, f32[768]{0:T(1024)}, u32[]{:S(2)}) copy-start(f32[768]{0:T(1024)} %copy-done.35) | copy-start | bytes 9220
  598.8 53.1 %copy-start.38 = (f32[1024]{0:T(1024)S(1)}, f32[1024]{0:T(1024)}, u32[]{:S(2)}) copy-start(f32[1024]{0:T(1024)} %copy-done.37) | copy-start | bytes 12292
  610.5 45.3 %copy-start.45 = (f32[1024]{0:T(1024)S(1)}, f32[1024]{0:T(1024)}, u32[]{:S(2)}) copy-start(f32[1024]{0:T(1024)} %copy-done.44) | copy-start | bytes 12292
  659.1 18.5 %copy-start.8 = (f32[1024,768]{0,1:T(8,128)S(1)}, f32[1024,768]{0,1:T(8,128)}, u32[]{:S(2)}) copy-start(f32[1024,768]{0,1:T(8,128)} %copy-done.7) | copy-start | bytes 9437188
  659.1 18.5 %copy-start.14 = (f32[1024,768]{0,1:T(8,128)S(1)}, f32[1024,768]{0,1:T(8,128)}, u32[]{:S(2)}) copy-start(f32[1024,768]{0,1:T(8,128)} %copy-done.13) | copy-start | bytes 9437188
  659.1 18.5 %copy-start.41 = (f32[1024]{0:T(1024)S(1)}, f32[1024]{0:T(1024)}, u32[]{:S(2)}) copy-start(f32[1024]{0:T(1024)} %copy-done.40) | copy-start | bytes 12292
  659.1 18.6 %copy-start.51 = (f32[768]{0:T(1024)S(1)}, f32[768]{0:T(1024)}, u32[]{:S(2)}) copy-start(f32[768]{0:T(1024)} %copy-done.50) | copy-start | bytes 9220
  659.1 18.6 %copy-start.58 = (f32[1024]{0:T(1024)S(1)}, f32[1024]{0:T(1024)}, u32[]{:S(2)}) copy-start(f32[1024]{0:T(1024)} %copy-done.57) | copy-start | bytes 12292
  677.7 9.9 copy-start.43
  693.2 385.8 %reduce-scatter.18.cloned.1.call-start = ((), (), s32[]{:S(2)}) async-start(), calls=%async_computation.16 | async-start | bytes 21233664 | tf_op jit(solution)/shard_map/reduce_scatter | solution.py:270
  710.6 9.3 copy-start.9
  710.6 9.3 copy-start.72
  763.2 24.5 %all-to-all-start.3 = ((bf16[1024,4,192]{0,2,1:T(8,128)(2,1)}), bf16[1024,4,192]{0,2,1:T(8,128)(2,1)}, u32[]{:S(2)}, u32[]{:S(2)}) async-start(bf16[1024,4,192]{0,2,1:T(8,128)(2,1)} %bitcast.483), calls=%async_computation.4 | async-start | bytes 3145728 | tf_op jit(solution)/shard_map/all_to_all | solution.py:208
  767.6 9.5 copy-start.63
  767.6 436.8 %all-reduce.3.cloned.1.call-start = ((), (), s32[]{:S(2)}) async-start(), calls=%async_computation.20 | async-start | bytes 147456 | tf_op jit(solution)/shard_map/psum | solution.py:288
  932.0 344.8 %reduce-scatter.22.cloned.1.call-start = ((), (), s32[]{:S(2)}) async-start(), calls=%async_computation.18 | async-start | bytes 1990656
  932.2 8.1 copy-start.29
  954.6 345.0 %reduce-scatter.24.cloned.1.call-start = ((), (), s32[]{:S(2)}) async-start(), calls=%async_computation.19 | async-start | bytes 491520
  957.0 403.6 %reduce-scatter.14.cloned.1.call-start = ((), (), s32[]{:S(2)}) async-start(), calls=%async_computation.14 | async-start | bytes 7864320 | tf_op jit(solution)/shard_map/reduce_scatter | solution.py:233
  966.8 429.4 %reduce-scatter.20.cloned.1.call-start = ((), (), s32[]{:S(2)}) async-start(), calls=%async_computation.17 | async-start | bytes 2949120 | tf_op jit(solution)/shard_map/reduce_scatter | solution.py:281
  1363.7 34.8 %copy-start.49 = (f32[2,3072]{1,0:T(2,128)S(1)}, f32[2,3072]{1,0:T(2,128)}, u32[]{:S(2)}) copy-start(f32[2,3072]{1,0:T(2,128)} %get-tuple-element.846) | copy-start | bytes 73732
  (35 other events, 100.5 us)
Sparse Core Ops, SparseCore 0:
  9.6 49.0 all-gather.2
  208.7 46.3 all-gather.4
  593.5 58.3 reduce-scatter.11
  693.3 69.0 reduce-scatter.15
  766.6 312.3 reduce-scatter.17
  1086.6 117.7 all-reduce.2
  1208.2 68.5 reduce-scatter.21
  1279.9 19.7 reduce-scatter.23
  1302.2 58.3 reduce-scatter.13
  1363.1 33.0 reduce-scatter.19
where the time goes:
time: 1420 us; the launch traced here: 1410 us
  waiting for transfers between devices  610 us (43%)
  matrix products  475 us (33%)
  local copies, waits for them, and re-layouts  185 us (13%)
  other arithmetic  102 us (7%)
  starting transfers between devices  17.2 us (1%)
  between operations  15.7 us (1%)
    psum x1, waiting for transfers between devices, on_device(): small_sum, shift_sum = lax.psum((small_stack, shift_stack), ('dp', 'head'))  123 us
    reduce_scatter x1, waiting for transfers between devices, on_device(): lax.psum_scatter(ffn_stack.astype(jnp.bfloat16), 'dp', scatter_dimension=...  112 us
    reduce_scatter x2, waiting for transfers between devices, on_device(): lax.psum_scatter(jnp.einsum('rce,cde->rd', grad_proj, layer_weights, pref...  101 us
    all_gather x2, waiting for transfers between devices, on_device(): lax.all_gather(hidden_state.astype(jnp.bfloat16), 'head', axis=0, tiled=T...  92.3 us
    unnamed x12, waiting for transfers between devices  89.2 us
    dot_general x2, matrix products, on_device(): jnp.dot(ffn_rows, up_part, preferred_element_type=jnp.float32) + up_shift  77.2 us
    unnamed x195, local copies, waits for them, and re-layouts  57.6 us
    dot_general x32, matrix products, slot_scores(): jnp.einsum('qhd,khd->hqk', queries, keys_in, preferred_element_type=jnp.f...  55.1 us
  transfers between devices with their start and end apart: 14, of which 13 were waited for; matrix products, arithmetic and copies ran while one was open for 21% of the time, Pallas kernels for 0%

commit v1 on v0

--- a/solution.py
+++ b/solution.py
@@ -285,7 +285,7 @@
             proj_data.astype(jnp.bfloat16), "head", scatter_dimension=2, tiled=True
         ).astype(jnp.float32),
     )
-    small_sum, shift_sum = lax.psum((small_stack, shift_stack), ("dp", "head"))
+    small_sum, shift_sum = lax.psum(lax.psum((small_stack, shift_stack), "head"), "dp")
     down_weight_grad = jnp.transpose(ffn_head[:, 1], (0, 2, 1))
     return (
         out_state,

time: 1420 us -> 1570 us (1.11)
  waiting for transfers between devices: 610 us -> 751 us
    reduce_scatter x1, waiting for transfers between devices: 112 us -> 304 us  [on_device(): lax.psum_scatter(ffn_stack.astype(jnp.bfloat16), 'dp', scatter_dimension=...]
    psum x1 -> x2, waiting for transfers between devices: 123 us -> 68.9 us  [the longest x1 68.9 us: on_device(): lax.psum(lax.psum((small_stack, shift_stack), 'head'), 'dp')]
    unnamed x12 -> x13, waiting for transfers between devices: 89.2 us -> 86.2 us
    unnamed x195 -> x175, local copies, waits for them, and re-layouts: 57.6 us -> 59.4 us
  transfers between devices with their start and end apart: 14 -> 15, of which waited for: 13 -> 14; matrix products, arithmetic and copies ran while one was open for 21% -> 11% of each run, Pallas kernels for 0% -> 0%
where the time goes in v1:
time: 1570 us; the launch traced here: 1550 us
  waiting for transfers between devices  751 us (48%)
  matrix products  475 us (30%)
  local copies, waits for them, and re-layouts  187 us (12%)
  other arithmetic  106 us (7%)
  starting transfers between devices  17.3 us (1%)
    reduce_scatter x1, waiting for transfers between devices, on_device(): lax.psum_scatter(ffn_stack.astype(jnp.bfloat16), 'dp', scatter_dimension=...  304 us
    reduce_scatter x2, waiting for transfers between devices, on_device(): lax.psum_scatter(jnp.einsum('rce,cde->rd', grad_proj, layer_weights, pref...  101 us
    all_gather x2, waiting for transfers between devices, on_device(): lax.all_gather(hidden_state.astype(jnp.bfloat16), 'head', axis=0, tiled=T...  92.3 us
    unnamed x13, waiting for transfers between devices  86.2 us
    dot_general x2, matrix products, on_device(): jnp.dot(ffn_rows, up_part, preferred_element_type=jnp.float32) + up_shift  77.2 us
    psum x1, waiting for transfers between devices, on_device(): lax.psum(lax.psum((small_stack, shift_stack), 'head'), 'dp')  68.9 us
    unnamed x175, local copies, waits for them, and re-layouts  59.4 us
    dot_general x32, matrix products, slot_scores(): jnp.einsum('qhd,khd->hqk', queries, keys_in, preferred_element_type=jnp.f...  55 us
  transfers between devices with their start and end apart: 15, of which 14 were waited for; matrix products, arithmetic and copies ran while one was open for 11% of the time, Pallas kernels for 0%

profile of v1, /device:TPU:0, one launch (start us, length us, event | category | flops | bytes accessed | tf_op | source)
XLA Modules:
  0.0 1552.8 jit_solution(5373393553655973951)
XLA Ops:
  12.9 45.8 %all-gather.3.cloned.1.call-done = bf16[4096,768]{1,0:T(8,128)(2,1)} async-done(((bf16[1024,768]{1,0:T(8,128)(2,1)}), bf16[4096,768]{1,0:T(8,128)(2,1)}) %all-gather.3.cloned.1.call-update) | async-done | bytes 6291472 | tf_op jit(solution)/shard_map/all_gather | solution.py:110
  58.7 6.0 fusion.216
  73.9 35.4 %while.52 = (s32[]{:T(128)}, bf16[8,512,3,64]{1,3,2,0:T(8,128)(2,1)}, f32[8,3,512]{2,1,0:T(4,128)S(1)}, bf16[8,512,3,64]{1,3,2,0:T(8,128)(2,1)}, s32[8,512]{1,0:...) while((s32[]{:T(128)}, ...), condition=%wide.region_5.6_spmd, body=%wide.region_2.5_spmd.sunk | while | flops 211122688 | bytes 11335773 | solution.py:123
  109.2 4.6 copy.159
  113.8 13.7 all_to_all.52
  130.6 3.7 all-to-all-start
  139.1 15.2 all-to-all-done
  154.4 4.0 fusion.212
  158.9 38.8 %multiply_convert_fusion.3 = (bf16[1024,3072]{1,0:T(8,128)(2,1)}, f32[1024,3072]{1,0:T(8,128)}, f32[1024,3072]{1,0:T(8,128)}) fusion(f32[3072]{0:T(1024)S(1)} %bitcast.494, bf16[2,768,3072]{2,1,0:T(8,128)(2,1)} %param.31, f32[1024,768]{0,1:T(8,128)S(1)} %get-tuple-element.480, f32[768]{0:T(1024)S(1)} %get-tuple-element.347, ...), kind=kOutput, calls=%fused_computation.148 | convolution fusion | flops 5043388416 | bytes 39348224 | tf_op jit(solution)/shard_map/dot_general | solution.py:139
  197.8 8.6 fusion.213
  208.6 46.5 %all-gather.5.cloned.1.call-done = bf16[4096,768]{0,1:T(8,128)(2,1)} async-done(((bf16[1024,768]{0,1:T(8,128)(2,1)}), bf16[4096,768]{0,1:T(8,128)(2,1)}) %all-gather.5.cloned.1.call-update) | async-done | bytes 6291472 | tf_op jit(solution)/shard_map/all_gather | solution.py:110
  255.2 6.6 fusion.217
  273.2 43.5 %while.53 = (s32[]{:T(128)}, bf16[8,512,3,64]{1,3,2,0:T(8,128)(2,1)}, f32[8,3,512]{2,1,0:T(4,128)S(1)}, bf16[8,512,3,64]{1,3,2,0:T(8,128)(2,1)}, s32[8,512]{1,0:...) while((s32[]{:T(128)}, ...), condition=%wide.region_13.14_spmd, body=%wide.region_10.13_spmd.sunk | while | flops 211122688 | bytes 11335773 | solution.py:123
  316.8 3.4 copy.165
  320.2 3.7 all_to_all.56
  327.0 4.6 all-to-all-start.1
  334.2 17.5 %all-to-all-done.1 = bf16[4,1024,192]{1,2,0:T(8,128)(2,1)} async-done(((bf16[4,1024,192]{1,2,0:T(8,128)(2,1)}), bf16[4,1024,192]{1,2,0:T(8,128)(2,1)}, u32[]{:S(2)}, u32[]{:S(2)}) %all-to-all-start.1) | async-done | bytes 1572896 | tf_op jit(solution)/shard_map/all_to_all | solution.py:127
  351.8 3.8 fusion.214
  356.4 38.4 %multiply_convert_fusion.2 = (bf16[1024,3072]{1,0:T(8,128)(2,1)}, f32[1024,3072]{1,0:T(8,128)}, f32[1024,3072]{1,0:T(8,128)}) fusion(f32[3072]{0:T(1024)S(1)} %bitcast.497, bf16[2,768,3072]{2,1,0:T(8,128)(2,1)} %param.31, f32[1024,768]{0,1:T(8,128)S(1)} %get-tuple-element.485, f32[768]{0:T(1024)S(1)} %copy-done.64, f32[768]{0:T(1024)S(1)} %copy-done.48, ...), kind=kOutput, calls=%fused_computation.135 | convolution fusion | flops 5043388416 | bytes 39348224 | tf_op jit(solution)/shard_map/dot_general | solution.py:139
  394.9 8.9 fusion.215
  409.3 17.6 %convert_reduce_fusion = (f32[3072]{0:T(1024)S(1)}, bf16[1024,3072]{1,0:T(8,128)(2,1)}) fusion(f32[1024,3072]{1,0:T(8,128)} %get-tuple-element.437, bf16[1024,768]{0,1:T(8,128)(2,1)S(1)} %get-tuple-element.427, bf16[2,3072,768]{2,1,0:T(8,128)(2,1)} %param.33, f32[1024,3072]{1,0:T(8,128)} %get-tuple-element.486, f32[3072]{0:T(1024)S(1)} %bitcast.498), kind=kOutput, calls=%fused_computation.131 | convolution fusion | flops 4885312512 | bytes 37773312 | tf_op jit(solution)/shard_map/rd,fd->rf/dot_general | solution.py:185
  426.9 11.1 multiply_reduce_fusion.2
  444.9 3.6 all-to-all-start.2
  448.5 20.0 %all-to-all-done.2 = bf16[1024,4,192]{0,2,1:T(8,128)(2,1)S(1)} async-done(((bf16[1024,4,192]{0,2,1:T(8,128)(2,1)}), bf16[1024,4,192]{0,2,1:T(8,128)(2,1)S(1)}, u32[]{:S(2)}, u32[]{:S(2)}) %all-to-all-start.2) | async-done | bytes 1572896 | tf_op jit(solution)/shard_map/all_to_all | solution.py:208
  476.6 88.1 %while.54 = (s32[]{:T(128)}, bf16[8,512,3,64]{1,3,2,0:T(8,128)(2,1)S(1)}, bf16[8,512,3,64]{1,3,2,0:T(8,128)(2,1)}, bf16[8,512,3,64]{1,3,2,0:T(8,128)(2,1)}, bf16...) while((s32[]{:T(128)}, ...), condition=%wide.region_24.25_spmd, body=%wide.region_22.24_spmd.sunk | while | flops 511146496 | bytes 26125428 | solution.py:210
  572.4 3.5 copy.174
  581.1 9.4 bitcast_convert_fusion.1
  591.9 4.0 fusion.172
  596.0 11.7 fusion.140
  607.7 41.4 %reduce-scatter.12.cloned.1.call-done = bf16[1024,768]{0,1:T(8,128)(2,1)} async-done(((bf16[4096,768]{0,1:T(8,128)(2,1)}), bf16[1024,768]{0,1:T(8,128)(2,1)}) %reduce-scatter.12.cloned.1.call-update) | async-done | bytes 1572880 | tf_op jit(solution)/shard_map/reduce_scatter | solution.py:233
  649.1 3.9 multiply_reduce_fusion.3
  656.5 18.5 %convert_reduce_fusion.1 = (f32[3072]{0:T(1024)S(1)}, bf16[1024,3072]{1,0:T(8,128)(2,1)}) fusion(f32[1024,3072]{1,0:T(8,128)} %get-tuple-element.439, bf16[1024,768]{0,1:T(8,128)(2,1)} %get-tuple-element.423, bf16[2,3072,768]{2,1,0:T(8,128)(2,1)} %param.33, f32[1024,3072]{1,0:T(8,128)} %get-tuple-element.481, f32[3072]{0:T(1024)S(1)} %bitcast.495), kind=kOutput, calls=%fused_computation.132 | convolution fusion | flops 4885312512 | bytes 37773312 | tf_op jit(solution)/shard_map/rd,fd->rf/dot_general | solution.py:185
  675.1 9.8 multiply_reduce_fusion.4
  690.5 4.4 all-to-all-start.3
  699.1 4.3 fusion.171
  703.5 11.6 all-to-all-done.3
  715.0 3.8 copy.177
  718.8 3.5 reshape.394
  729.4 101.6 %while.55 = (s32[]{:T(128)}, bf16[8,512,3,64]{1,3,2,0:T(8,128)(2,1)}, bf16[8,512,3,64]{1,3,2,0:T(8,128)(2,1)}, bf16[8,512,3,64]{1,3,2,0:T(8,128)(2,1)}, bf16[8,5...) while((s32[]{:T(128)}, ...), condition=%wide.region_32.33_spmd, body=%wide.region_30.32_spmd.sunk | while | flops 511146496 | bytes 26125428 | solution.py:210
  831.0 3.4 copy.179
  834.4 3.8 stack.140
  843.0 3.8 stack.141
  846.8 3.4 copy.181
  850.2 3.8 stack.142
  862.4 3.2 pad_maximum_fusion.1
  865.7 9.0 fusion.141
  874.7 8.4 maximum_bitcast_fusion.1
  883.1 9.3 fusion.139
  892.4 9.8 fusion.138
  902.1 8.5 maximum_bitcast_fusion
  910.6 16.7 %pad_maximum_fusion = bf16[2,2,768,3072]{3,2,1,0:T(8,128)(2,1)} fusion(bf16[1,2,768,3072]{3,2,1,0:T(8,128)(2,1)} %maximum_bitcast_fusion.1, bf16[1,2,768,3072]{3,2,1,0:T(8,128)(2,1)} %maximum_bitcast_fusion), kind=kLoop, calls=%fused_computation.126 | loop fusion | flops 9437184 | bytes 37748736 | tf_op jit(solution)/shard_map/stack | solution.py:264
  927.7 9.1 fusion.173
  936.8 9.1 fusion.176
  948.8 5.9 copy.207
  954.7 6.9 reshape.411
  961.7 4.7 reduce-scatter.16.cloned.1.call-done
  968.7 9.5 bitcast_convert_fusion
  978.5 304.0 %reduce-scatter.18.cloned.1.call-done = bf16[2,2,96,3072]{3,2,1,0:T(8,128)(2,1)} async-done(((bf16[2,2,768,3072]{3,2,1,0:T(8,128)(2,1)}), bf16[2,2,96,3072]{3,2,1,0:T(8,128)(2,1)}) %reduce-scatter.18.cloned.1.call-update) | async-done | bytes 2359312 | tf_op jit(solution)/shard_map/reduce_scatter | solution.py:270
  1285.1 68.9 %all-reduce.5.cloned.1.call-done = (f32[2,8,768]{2,0,1:T(2,128)}, f32[2,3072]{1,0:T(2,128)}) async-done(((f32[2,8,768]{2,0,1:T(2,128)}, f32[2,3072]{1,0:T(2,128)}), (f32[2,8,768]{2,0,1:T(2,128)}, f32[2,3072]{1,0:T(2,128)})) %all-reduce.5.cloned.1.call-update) | async-done | bytes 73744 | tf_op jit(solution)/shard_map/psum | solution.py:288
  1356.7 66.7 %reduce-scatter.22.cloned.1.call-done = bf16[96,1152]{1,0:T(8,128)(2,1)} async-done(((bf16[768,1152]{1,0:T(8,128)(2,1)}), bf16[96,1152]{1,0:T(8,128)(2,1)}) %reduce-scatter.22.cloned.1.call-update) | async-done | bytes 221200
  1427.6 18.7 %reduce-scatter.24.cloned.1.call-done = bf16[192,192]{1,0:T(8,128)(2,1)} async-done(((bf16[768,192]{1,0:T(8,128)(2,1)}), bf16[192,192]{1,0:T(8,128)(2,1)}) %reduce-scatter.24.cloned.1.call-update) | async-done | bytes 73744
  1448.1 59.1 %reduce-scatter.14.cloned.1.call-done = bf16[1024,768]{0,1:T(8,128)(2,1)} async-done(((bf16[4096,768]{0,1:T(8,128)(2,1)}), bf16[1024,768]{0,1:T(8,128)(2,1)}) %reduce-scatter.14.cloned.1.call-update) | async-done | bytes 1572880 | tf_op jit(solution)/shard_map/reduce_scatter | solution.py:233
  1507.3 3.1 add_convert_fusion.4
  1513.0 29.9 %reduce-scatter.20.cloned.1.call-done = bf16[2,2,96,768]{3,2,1,0:T(8,128)(2,1)} async-done(((bf16[2,2,96,3072]{3,2,1,0:T(8,128)(2,1)}), bf16[2,2,96,768]{3,2,1,0:T(8,128)(2,1)}) %reduce-scatter.20.cloned.1.call-update) | async-done | bytes 589840 | tf_op jit(solution)/shard_map/reduce_scatter | solution.py:281
  (542 shorter events, 401.7 us)
Async XLA Ops:
  7.2 51.5 %all-gather.3.cloned.1.call-start = ((), (), s32[]{:S(2)}) async-start(), calls=%async_computation.11 | async-start | bytes 7864320 | tf_op jit(solution)/shard_map/all_gather | solution.py:110
  109.2 18.3 %copy-start.5 = (bf16[8,512,3,64]{1,3,2,0:T(8,128)(2,1)}, bf16[8,512,3,64]{1,3,2,0:T(8,128)(2,1)S(1)}, u32[]{:S(2)}) copy-start(bf16[8,512,3,64]{1,3,2,0:T(8,128)(2,1)S(1)} %get-tuple-element.872) | copy-start | bytes 4718596
  109.2 18.3 %copy-start.6 = (bf16[8,512,3,64]{1,3,2,0:T(8,128)(2,1)}, bf16[8,512,3,64]{1,3,2,0:T(8,128)(2,1)S(1)}, u32[]{:S(2)}) copy-start(bf16[8,512,3,64]{1,3,2,0:T(8,128)(2,1)S(1)} %get-tuple-element.873) | copy-start | bytes 4718596
  109.2 18.3 %copy-start.27 = (f32[8,3,512]{2,1,0:T(4,128)}, f32[8,3,512]{2,1,0:T(4,128)S(1)}, u32[]{:S(2)}) copy-start(f32[8,3,512]{2,1,0:T(4,128)S(1)} %get-tuple-element.813) | copy-start | bytes 147460
  130.6 6.7 copy-start.58
  130.6 7.3 copy-start.60
  130.6 7.3 copy-start.61
  130.6 7.9 copy-start.44
  130.6 23.8 %all-to-all-start = ((bf16[4,1024,192]{1,2,0:T(8,128)(2,1)}), bf16[4,1024,192]{1,2,0:T(8,128)(2,1)S(1)}, u32[]{:S(2)}, u32[]{:S(2)}) async-start(bf16[4,1024,192]{1,2,0:T(8,128)(2,1)} %copy.160), calls=%async_computation | async-start | bytes 3145728 | tf_op jit(solution)/shard_map/all_to_all | solution.py:127
  134.3 120.8 %all-gather.5.cloned.1.call-start = ((), (), s32[]{:S(2)}) async-start(), calls=%async_computation.12 | async-start | bytes 7864320 | tf_op jit(solution)/shard_map/all_gather | solution.py:110
  137.9 59.8 %copy-start.46 = (f32[768]{0:T(1024)}, f32[768]{0:T(1024)S(1)}, u32[]{:S(2)}) copy-start(f32[768]{0:T(1024)S(1)} %get-tuple-element.497) | copy-start | bytes 9220
  137.9 59.8 %copy-start.62 = (f32[768]{0:T(1024)}, f32[768]{0:T(1024)S(1)}, u32[]{:S(2)}) copy-start(f32[768]{0:T(1024)S(1)} %get-tuple-element.347) | copy-start | bytes 9220
  138.5 213.2 %copy-start.31 = (f32[768]{0:T(1024)}, f32[768]{0:T(1024)S(1)}, u32[]{:S(2)}) copy-start(f32[768]{0:T(1024)S(1)} %get-tuple-element.499) | copy-start | bytes 9220
  139.1 19.7 %copy-start.53 = (f32[1,3072]{1,0:T(1,128)}, f32[1,3072]{1,0:T(1,128)S(1)}, u32[]{:S(2)}) copy-start(f32[1,3072]{1,0:T(1,128)S(1)} %get-tuple-element.466) | copy-start | bytes 36868
  154.4 43.4 %slice-start = ((s8[9437184]{0:T(1024)(128)(4,1)}), s8[4194304]{0:T(1024)(128)(4,1)S(1)}, s32[]{:S(2)}) async-start(s8[9437184]{0:T(1024)(128)(4,1)} %bitcast.500), calls=%async_computation.22 | async-start | bytes 8388608
  158.4 39.3 %copy-start.7 = (f32[1024,768]{0,1:T(8,128)}, f32[1024,768]{0,1:T(8,128)S(1)}, u32[]{:S(2)}) copy-start(f32[1024,768]{0,1:T(8,128)S(1)} %get-tuple-element.480) | copy-start | bytes 9437188
  158.4 39.3 %copy-start.36 = (f32[1024]{0:T(1024)}, f32[1024]{0:T(1024)S(1)}, u32[]{:S(2)}) copy-start(f32[1024]{0:T(1024)S(1)} %broadcast_multiply_fusion.3) | copy-start | bytes 12292
  158.8 38.8 %copy-start.38 = (f32[1024]{0:T(1024)}, f32[1024]{0:T(1024)S(1)}, u32[]{:S(2)}) copy-start(f32[1024]{0:T(1024)S(1)} %multiply_reduce_fusion.11) | copy-start | bytes 12292
  158.9 38.9 %copy-start.50 = (f32[1024]{0:T(1024)}, f32[1024]{0:T(1024)S(1)}, u32[]{:S(2)}) copy-start(f32[1024]{0:T(1024)S(1)} %fusion.189) | copy-start | bytes 12292
  158.9 38.9 %slice-start.1 = ((s8[9437184]{0:T(1024)(128)(4,1)}), s8[4194304]{0:T(1024)(128)(4,1)S(1)}, s32[]{:S(2)}) async-start(s8[9437184]{0:T(1024)(128)(4,1)} %bitcast.500), calls=%async_computation.23 | async-start | bytes 8388608
  158.9 38.9 %slice-start.2 = ((s8[9437184]{0:T(1024)(128)(4,1)}), s8[1048576]{0:T(1024)(128)(4,1)S(1)}, s32[]{:S(2)}) async-start(s8[9437184]{0:T(1024)(128)(4,1)} %bitcast.500), calls=%async_computation.24 | async-start | bytes 2097152
  206.4 145.3 %copy-start = (f32[1024,768]{0,1:T(8,128)}, f32[1024,768]{0,1:T(8,128)S(1)}, u32[]{:S(2)}) copy-start(f32[1024,768]{0,1:T(8,128)S(1)} %get-tuple-element.483) | copy-start | bytes 9437188
  206.4 145.3 %copy-start.29 = (f32[1024]{0:T(1024)}, f32[1024]{0:T(1024)S(1)}, u32[]{:S(2)}) copy-start(f32[1024]{0:T(1024)S(1)} %broadcast_multiply_fusion.2) | copy-start | bytes 12292
  206.8 144.9 %copy-start.33 = (f32[1024]{0:T(1024)}, f32[1024]{0:T(1024)S(1)}, u32[]{:S(2)}) copy-start(f32[1024]{0:T(1024)S(1)} %fusion.190) | copy-start | bytes 12292
  316.8 7.2 copy-start.26
  316.8 7.2 copy-start.28
  327.0 24.8 %copy-start.66 = (f32[768]{0:T(1024)S(1)}, f32[768]{0:T(1024)}, u32[]{:S(2)}) copy-start(f32[768]{0:T(1024)} %get-tuple-element.348) | copy-start | bytes 9220
  327.0 24.8 %all-to-all-start.1 = ((bf16[4,1024,192]{1,2,0:T(8,128)(2,1)}), bf16[4,1024,192]{1,2,0:T(8,128)(2,1)}, u32[]{:S(2)}, u32[]{:S(2)}) async-start(bf16[4,1024,192]{1,2,0:T(8,128)(2,1)} %copy.166), calls=%async_computation.1 | async-start | bytes 3145728 | tf_op jit(solution)/shard_map/all_to_all | solution.py:127
  351.8 43.1 %slice-start.3 = ((s8[9437184]{0:T(1024)(128)(4,1)}), s8[4194304]{0:T(1024)(128)(4,1)S(1)}, s32[]{:S(2)}) async-start(s8[9437184]{0:T(1024)(128)(4,1)} %bitcast.502), calls=%async_computation.25 | async-start | bytes 8388608
  355.6 39.3 %copy-start.10 = (f32[1024,768]{0,1:T(8,128)}, f32[1024,768]{0,1:T(8,128)S(1)}, u32[]{:S(2)}) copy-start(f32[1024,768]{0,1:T(8,128)S(1)} %get-tuple-element.485) | copy-start | bytes 9437188
  356.0 38.8 %copy-start.42 = (f32[1024]{0:T(1024)}, f32[1024]{0:T(1024)S(1)}, u32[]{:S(2)}) copy-start(f32[1024]{0:T(1024)S(1)} %multiply_reduce_fusion.9) | copy-start | bytes 12292
  356.4 38.5 %copy-start.65 = (f32[768]{0:T(1024)S(1)}, f32[768]{0:T(1024)}, u32[]{:S(2)}) copy-start(f32[768]{0:T(1024)} %get-tuple-element.342) | copy-start | bytes 9220
  356.4 38.5 %slice-start.4 = ((s8[9437184]{0:T(1024)(128)(4,1)}), s8[4194304]{0:T(1024)(128)(4,1)S(1)}, s32[]{:S(2)}) async-start(s8[9437184]{0:T(1024)(128)(4,1)} %bitcast.502), calls=%async_computation.26 | async-start | bytes 8388608
  356.4 38.5 %slice-start.5 = ((s8[9437184]{0:T(1024)(128)(4,1)}), s8[1048576]{0:T(1024)(128)(4,1)S(1)}, s32[]{:S(2)}) async-start(s8[9437184]{0:T(1024)(128)(4,1)} %bitcast.502), calls=%async_computation.27 | async-start | bytes 2097152
  394.9 8.9 copy-start.4
  394.9 8.9 copy-start.35
  409.3 17.6 %copy-start.22 = (bf16[1024,768]{0,1:T(8,128)(2,1)}, bf16[1024,768]{0,1:T(8,128)(2,1)S(1)}, u32[]{:S(2)}) copy-start(bf16[1024,768]{0,1:T(8,128)(2,1)S(1)} %get-tuple-element.427) | copy-start | bytes 4718596
  426.9 11.1 copy-start.43
  426.9 11.2 copy-start.11
  444.9 23.6 %all-to-all-start.2 = ((bf16[1024,4,192]{0,2,1:T(8,128)(2,1)}), bf16[1024,4,192]{0,2,1:T(8,128)(2,1)S(1)}, u32[]{:S(2)}, u32[]{:S(2)}) async-start(bf16[1024,4,192]{0,2,1:T(8,128)(2,1)} %bitcast.68), calls=%async_computation.2 | async-start | bytes 3145728 | tf_op jit(solution)/shard_map/all_to_all | solution.py:208
  448.5 200.6 %reduce-scatter.12.cloned.1.call-start = ((), (), s32[]{:S(2)}) async-start(), calls=%async_computation.13 | async-start | bytes 7864320 | tf_op jit(solution)/shard_map/reduce_scatter | solution.py:233
  596.0 53.1 %copy-start.1 = (f32[1024,768]{0,1:T(8,128)S(1)}, f32[1024,768]{0,1:T(8,128)}, u32[]{:S(2)}) copy-start(f32[1024,768]{0,1:T(8,128)} %copy-done) | copy-start | bytes 9437188
  596.0 53.1 %copy-start.30 = (f32[1024]{0:T(1024)S(1)}, f32[1024]{0:T(1024)}, u32[]{:S(2)}) copy-start(f32[1024]{0:T(1024)} %copy-done.29) | copy-start | bytes 12292
  596.0 53.1 %copy-start.32 = (f32[768]{0:T(1024)S(1)}, f32[768]{0:T(1024)}, u32[]{:S(2)}) copy-start(f32[768]{0:T(1024)} %copy-done.31) | copy-start | bytes 9220
  596.0 53.1 %copy-start.34 = (f32[1024]{0:T(1024)S(1)}, f32[1024]{0:T(1024)}, u32[]{:S(2)}) copy-start(f32[1024]{0:T(1024)} %copy-done.33) | copy-start | bytes 12292
  607.7 45.3 %copy-start.41 = (f32[1024]{0:T(1024)S(1)}, f32[1024]{0:T(1024)}, u32[]{:S(2)}) copy-start(f32[1024]{0:T(1024)} %copy-done.40) | copy-start | bytes 12292
  656.5 18.6 %copy-start.8 = (f32[1024,768]{0,1:T(8,128)S(1)}, f32[1024,768]{0,1:T(8,128)}, u32[]{:S(2)}) copy-start(f32[1024,768]{0,1:T(8,128)} %copy-done.7) | copy-start | bytes 9437188
  656.5 18.6 %copy-start.14 = (f32[1024,768]{0,1:T(8,128)S(1)}, f32[1024,768]{0,1:T(8,128)}, u32[]{:S(2)}) copy-start(f32[1024,768]{0,1:T(8,128)} %copy-done.13) | copy-start | bytes 9437188
  656.5 18.6 %copy-start.37 = (f32[1024]{0:T(1024)S(1)}, f32[1024]{0:T(1024)}, u32[]{:S(2)}) copy-start(f32[1024]{0:T(1024)} %copy-done.36) | copy-start | bytes 12292
  656.5 18.6 %copy-start.47 = (f32[768]{0:T(1024)S(1)}, f32[768]{0:T(1024)}, u32[]{:S(2)}) copy-start(f32[768]{0:T(1024)} %copy-done.46) | copy-start | bytes 9220
  656.5 18.6 %copy-start.51 = (f32[1024]{0:T(1024)S(1)}, f32[1024]{0:T(1024)}, u32[]{:S(2)}) copy-start(f32[1024]{0:T(1024)} %copy-done.50) | copy-start | bytes 12292
  675.1 9.8 copy-start.39
  690.5 24.5 %all-to-all-start.3 = ((bf16[1024,4,192]{0,2,1:T(8,128)(2,1)}), bf16[1024,4,192]{0,2,1:T(8,128)(2,1)}, u32[]{:S(2)}, u32[]{:S(2)}) async-start(bf16[1024,4,192]{0,2,1:T(8,128)(2,1)} %bitcast.483), calls=%async_computation.4 | async-start | bytes 3145728 | tf_op jit(solution)/shard_map/all_to_all | solution.py:208
  694.9 251.0 %all-reduce.7.cloned.1.call-start = ((), (), s32[]{:S(2)}) async-start(), calls=%async_computation.21 | async-start | bytes 147456 | tf_op jit(solution)/shard_map/psum | solution.py:288
  862.3 104.1 %reduce-scatter.16.cloned.1.call-start = ((), (), s32[]{:S(2)}) async-start(), calls=%async_computation.15 | async-start | bytes 2654208 | tf_op jit(solution)/shard_map/reduce_scatter | solution.py:273
  865.6 416.9 %reduce-scatter.18.cloned.1.call-start = ((), (), s32[]{:S(2)}) async-start(), calls=%async_computation.16 | async-start | bytes 21233664 | tf_op jit(solution)/shard_map/reduce_scatter | solution.py:270
  883.1 9.3 copy-start.9
  883.1 9.3 copy-start.63
  927.4 426.6 %all-reduce.5.cloned.1.call-start = ((), (), s32[]{:S(2)}) async-start(), calls=%async_computation.20 | async-start | bytes 147456 | tf_op jit(solution)/shard_map/psum | solution.py:288
  945.9 477.5 %reduce-scatter.22.cloned.1.call-start = ((), (), s32[]{:S(2)}) async-start(), calls=%async_computation.18 | async-start | bytes 1990656
  961.7 484.7 %reduce-scatter.24.cloned.1.call-start = ((), (), s32[]{:S(2)}) async-start(), calls=%async_computation.19 | async-start | bytes 491520
  968.6 538.6 %reduce-scatter.14.cloned.1.call-start = ((), (), s32[]{:S(2)}) async-start(), calls=%async_computation.14 | async-start | bytes 7864320 | tf_op jit(solution)/shard_map/reduce_scatter | solution.py:233
  978.2 564.7 %reduce-scatter.20.cloned.1.call-start = ((), (), s32[]{:S(2)}) async-start(), calls=%async_computation.17 | async-start | bytes 2949120 | tf_op jit(solution)/shard_map/reduce_scatter | solution.py:281
  1510.4 34.8 %copy-start.45 = (f32[2,3072]{1,0:T(2,128)S(1)}, f32[2,3072]{1,0:T(2,128)}, u32[]{:S(2)}) copy-start(f32[2,3072]{1,0:T(2,128)} %get-tuple-element.848) | copy-start | bytes 73732
  (26 other events, 90.3 us)
Sparse Core Ops, SparseCore 0:
  9.6 49.0 all-gather.2
  208.7 46.3 all-gather.4
  590.7 58.3 reduce-scatter.11
  862.4 29.4 all-reduce.6
  895.3 71.0 reduce-scatter.15
  970.1 312.3 reduce-scatter.17
  1286.1 67.8 all-reduce.4
  1357.5 65.8 reduce-scatter.21
  1426.6 19.6 reduce-scatter.23
  1448.9 58.3 reduce-scatter.13
  1509.8 33.0 reduce-scatter.19
